TPU v7x, 32 devices: a whole 2x2x4 slice. The times are simulated.
32 devices in a mesh: grp: 2 (over x), tile: 16 (over z, y, core).
Axes of the slice: x: 2, y: 2, z: 4, core: 2. Of those that a mesh axis runs over, the one named last changes fastest.
Arguments:
- voltages: bfloat16 [2, 32, 128, 1024], P(None, ('grp', 'tile')), parts along dimension 1, may hold values from -6 to 6
Outputs:
- visibilities: float32 [2, 2, 136, 128, 128], P(None, 'grp', None, 'tile'), parts along dimension 1
There are 2 independent parts, one for each index of `grp`. A program takes and returns all parts, laid end to end along the dimension named above; each array names one. Nothing has to cross between parts.
All inputs are finite; a program needn't handle non-finite values.
Results may differ from a plain program's by a relative error of at most 0.0003.
Values may be sent and summed in bfloat16 or wider, within the bound.
No kernel may reach another device: no remote copies, remote signals or barrier semaphores. Data moves between devices by JAX's collectives and lax.ppermute only.
A program may use at most 64 MiB of HBM per device.

v0:
```python
import jax
import jax.numpy as jnp
import numpy as np
from jax import lax
from jax.sharding import PartitionSpec as P

NBLK = 16
TIME = 1024


def passed_along(block, axis, distance):
    devices = range(lax.axis_size(axis))
    route = [((i - distance) % len(devices), i) for i in devices]
    return lax.ppermute(block, axis, route)


def pair_tile(rows_side, cols_side):
    real_part = jnp.einsum(
        "cit,cjt->cij", rows_side[0], cols_side[0], preferred_element_type=jnp.float32
    ) + jnp.einsum("cit,cjt->cij", rows_side[1], cols_side[1], preferred_element_type=jnp.float32)
    imag_part = jnp.einsum(
        "cit,cjt->cij", rows_side[1], cols_side[0], preferred_element_type=jnp.float32
    ) - jnp.einsum("cit,cjt->cij", rows_side[0], cols_side[1], preferred_element_type=jnp.float32)
    return jnp.stack([real_part, imag_part]) / TIME


def covers_all(members, blocks_count):
    reached = set()
    for first_member in members:
        for second_member in members:
            reached.add((first_member - second_member) % blocks_count)
    return len(reached) == blocks_count


def search_cover(members, first_value, target_count, blocks_count):
    if len(members) == target_count:
        if covers_all(members, blocks_count):
            return members
        return []
    for candidate in range(first_value, blocks_count):
        outcome = search_cover(members + [candidate], candidate + 1, target_count, blocks_count)
        if outcome:
            return outcome
    return []


def cover_offsets(blocks_count):
    target_count = 2
    while target_count <= blocks_count:
        outcome = search_cover([0], 1, target_count, blocks_count)
        if outcome:
            return outcome
        target_count = target_count + 1
    return list(range(blocks_count))


def class_pair(members, distance, blocks_count):
    for first_member in members:
        for second_member in members:
            if (second_member - first_member) % blocks_count == distance:
                return (first_member, second_member)
    return (0, distance)


def cover_sources(stride, members):
    sources = []
    for row_block in range(NBLK):
        for col_block in range(row_block, NBLK):
            if row_block == col_block:
                sources.append(row_block * stride)
            else:
                gap_size = col_block - row_block
                distance = min(gap_size, NBLK - gap_size)
                first_member, second_member = class_pair(members, distance, NBLK)
                if gap_size == distance:
                    owner_block = (row_block - first_member) % NBLK
                else:
                    owner_block = (col_block - first_member) % NBLK
                sources.append(owner_block * stride + distance)
    return np.array(sources, np.int32)


def channel_order(received, slot_count, sources):
    rows_part = received.shape[4]
    width = received.shape[5]
    all_channels = received.shape[1] * received.shape[2] // NBLK
    arranged = received.reshape(2, NBLK, all_channels, slot_count, rows_part, width)
    arranged = jnp.transpose(arranged, (0, 2, 1, 3, 4, 5)).reshape(
        2, all_channels, NBLK * slot_count, rows_part, width
    )
    return jnp.take(arranged, jnp.asarray(sources), axis=2)


def on_device(voltages):
    split_count = lax.axis_size("tile") // NBLK
    own_block = lax.axis_index("tile") // split_count
    diagonal = pair_tile(voltages, voltages)
    members = cover_offsets(NBLK)
    fetched = {0: voltages}
    for member_offset in members[1:]:
        fetched[member_offset] = passed_along(voltages, "tile", -member_offset * split_count)
    tiles_list = [diagonal]
    for distance in range(1, NBLK // 2 + 1):
        first_member, second_member = class_pair(members, distance, NBLK)
        product = pair_tile(fetched[first_member], fetched[second_member])
        flipped = jnp.stack([jnp.swapaxes(product[0], 1, 2), -jnp.swapaxes(product[1], 1, 2)])
        first_block = (own_block + first_member) % NBLK
        second_block = (own_block + second_member) % NBLK
        tiles_list.append(jnp.where(first_block < second_block, product, flipped))
    tile_slots = jnp.stack(tiles_list, axis=2)
    received = lax.all_to_all(tile_slots[:, None], "tile", split_axis=4, concat_axis=1, tiled=True)
    return channel_order(received, NBLK // 2 + 1, cover_sources(NBLK // 2 + 1, members))


def solution(mesh):
    placed = (P(None, ("grp", "tile"), None, None),)
    return jax.shard_map(
        on_device,
        mesh=mesh,
        in_specs=placed,
        out_specs=P(None, "grp", None, "tile", None),
        check_vma=False,
    )
```

profile of v0, /device:TPU:15, one launch (start us, length us, event | category | flops | bytes accessed | tf_op | source)
XLA Modules:
  0.0 124.3 jit_solution(4143550448847985932)
XLA Ops:
  0.0 0.7 collective-permute-start
  0.7 0.2 collective-permute-start.1
  0.9 4.3 %collective-permute-start.2 = (bf16[2,1,128,1024]{3,2,1,0:T(8,128)(2,1)}, bf16[2,1,128,1024]{3,2,1,0:T(8,128)(2,1)}, u32[]{:S(2)}, u32[]{:S(2)}) collective-permute-start(bf16[2,1,128,1024]{3,2,1,0:T(8,128)(2,1)} %param.2), channel_id=1, source_target_pairs={{5,0},{6,1},{7,2},{8,3},{9,4},{10,5},{11,6},{12,7},{13,8},{14,9},{... | collective-permute-start | bytes 1572872 | tf_op jit(solution)/shard_map/ppermute | solution.py:14
  5.2 0.0 collective-permute-start.3
  5.2 1.3 %fusion.32 = f32[128,128]{1,0:T(8,128)S(1)} fusion(bf16[2,1,128,1024]{3,2,1,0:T(8,128)(2,1)} %param.2), kind=kOutput, calls=%fused_computation.60 | convolution fusion | flops 33554432 | bytes 327680 | tf_op jit(solution)/shard_map/cit,cjt->cij/dot_general | solution.py:18
  6.5 1.3 %fusion.1 = f32[1,1,1,128,128]{4,3,2,1,0:T(8,128)S(1)} fusion(f32[128,128]{1,0:T(8,128)S(1)} %fusion.32, bf16[2,1,128,1024]{3,2,1,0:T(8,128)(2,1)} %param.2), kind=kOutput, calls=%fused_computation.21 | convolution fusion | flops 33570816 | bytes 393216 | tf_op jit(solution)/shard_map/cit,cjt->cij/dot_general | solution.py:20
  7.9 1.3 %fusion.15 = f32[128,128]{1,0:T(8,128)S(1)} fusion(bf16[2,1,128,1024]{3,2,1,0:T(8,128)(2,1)} %param.2), kind=kOutput, calls=%fused_computation.43 | convolution fusion | flops 33554432 | bytes 589824 | tf_op jit(solution)/shard_map/cit,cjt->cij/dot_general | solution.py:21
  9.1 0.0 copy-done.1
  9.1 0.2 fusion
  9.4 5.8 %collective-permute-done = bf16[2,1,128,1024]{3,2,1,0:T(8,128)(2,1)S(1)} collective-permute-done((bf16[2,1,128,1024]{3,2,1,0:T(8,128)(2,1)}, bf16[2,1,128,1024]{3,2,1,0:T(8,128)(2,1)S(1)}, u32[]{:S(2)}, u32[]{:S(2)}) %collective-permute-start) | collective-permute-done | bytes 524320 | tf_op jit(solution)/shard_map/ppermute | solution.py:14
  15.2 0.2 fusion.12
  15.5 0.2 convolution_add_fusion.7
  15.7 0.2 fusion.27
  15.9 0.2 convolution_subtract_fusion.7
  16.2 0.1 copy.143
  16.3 2.3 %collective-permute-done.1 = bf16[2,1,128,1024]{3,2,1,0:T(8,128)(2,1)S(1)} collective-permute-done((bf16[2,1,128,1024]{3,2,1,0:T(8,128)(2,1)}, bf16[2,1,128,1024]{3,2,1,0:T(8,128)(2,1)S(1)}, u32[]{:S(2)}, u32[]{:S(2)}) %collective-permute-start.1) | collective-permute-done | bytes 524320 | tf_op jit(solution)/shard_map/ppermute | solution.py:14
  18.6 0.2 fusion.9
  18.8 0.2 fusion.24
  19.0 0.2 convolution_add_fusion.6
  19.3 0.2 convolution_subtract_fusion.6
  19.5 0.1 copy.148
  19.7 19.2 %collective-permute-done.2 = bf16[2,1,128,1024]{3,2,1,0:T(8,128)(2,1)} collective-permute-done((bf16[2,1,128,1024]{3,2,1,0:T(8,128)(2,1)}, bf16[2,1,128,1024]{3,2,1,0:T(8,128)(2,1)}, u32[]{:S(2)}, u32[]{:S(2)}) %collective-permute-start.2) | collective-permute-done | bytes 524320 | tf_op jit(solution)/shard_map/ppermute | solution.py:14
  38.9 1.2 fusion.52
  40.1 1.2 fusion.50
  41.3 1.2 convolution_add_fusion.5
  42.5 0.0 copy-done.3
  42.5 1.2 convolution_subtract_fusion.5
  43.7 0.1 copy.153
  43.8 1.2 fusion.48
  45.0 1.2 fusion.46
  46.2 1.2 convolution_add_fusion.4
  47.4 1.2 convolution_subtract_fusion.4
  48.6 0.1 copy.158
  48.7 1.2 fusion.6
  49.9 1.2 fusion.21
  51.1 1.2 convolution_add_fusion.3
  52.3 1.2 convolution_subtract_fusion.3
  53.5 0.1 copy.163
  53.6 0.0 copy-start.4
  53.7 0.0 collective-permute-done.3
  53.7 1.3 %fusion.51 = f32[128,128]{0,1:T(8,128)S(1)} fusion(bf16[2,1,128,1024]{3,2,1,0:T(8,128)(2,1)} %copy-done.3, bf16[2,1,128,1024]{3,2,1,0:T(8,128)(2,1)} %collective-permute-done.3), kind=kOutput, calls=%fused_computation.102 | convolution fusion | flops 33554432 | bytes 589824 | tf_op jit(solution)/shard_map/cit,cjt->cij/dot_general | solution.py:20
  55.0 0.0 copy-done.4
  55.0 1.2 fusion.49
  56.2 1.2 convolution_add_fusion.2
  57.4 1.2 convolution_subtract_fusion.2
  58.6 0.1 copy.168
  58.7 1.2 fusion.47
  59.9 1.2 fusion.45
  61.1 1.2 convolution_add_fusion.1
  62.3 1.2 convolution_subtract_fusion.1
  63.5 0.1 copy.169
  63.6 0.0 copy-start.2
  63.7 1.3 %fusion.3 = f32[128,128]{1,0:T(8,128)S(1)} fusion(bf16[2,1,128,1024]{3,2,1,0:T(8,128)(2,1)} %collective-permute-done.3, bf16[2,1,128,1024]{3,2,1,0:T(8,128)(2,1)} %param.2), kind=kOutput, calls=%fused_computation.31 | convolution fusion | flops 33554432 | bytes 589824 | tf_op jit(solution)/shard_map/cit,cjt->cij/dot_general | solution.py:20
  65.0 1.2 fusion.18
  66.2 1.2 convolution_add_fusion
  67.4 1.2 convolution_subtract_fusion
  68.6 0.1 copy.170
  68.9 2.0 %copy.171 = f32[2,1,1,9,128,128]{5,0,3,2,1,4:T(2,128)} copy(f32[2,1,1,9,128,128]{5,4,3,0,2,1:T(8,128)S(1)} %bitcast.255) | data formatting | bytes 2359296 | tf_op jit(solution)/shard_map/broadcast_in_dim | solution.py:111
  70.9 23.7 %all-to-all-start = ((f32[2,1,1,9,128,128]{5,0,3,2,1,4:T(2,128)}), f32[2,1,1,9,128,128]{5,0,3,2,1,4:T(2,128)S(1)}, u32[]{:S(2)}, u32[]{:S(2)}) async-start(f32[2,1,1,9,128,128]{5,0,3,2,1,4:T(2,128)} %copy.171), calls=%async_computation | async-start | bytes 2359296 | tf_op jit(solution)/shard_map/all_to_all | solution.py:111
  94.6 27.7 %all-to-all-done = f32[2,1,1,9,128,128]{5,0,3,2,1,4:T(2,128)S(1)} async-done(((f32[2,1,1,9,128,128]{5,0,3,2,1,4:T(2,128)}), f32[2,1,1,9,128,128]{5,0,3,2,1,4:T(2,128)S(1)}, u32[]{:S(2)}, u32[]{:S(2)}) %all-to-all-start) | async-done | bytes 1179680 | tf_op jit(solution)/shard_map/all_to_all | solution.py:111
  122.3 0.1 copy.200
  122.5 0.1 copy.173
  122.6 0.7 gather_fusion
  123.3 1.1 copy.174
  (39 shorter events, 0.5 us)
Async XLA Ops:
  0.0 9.1 %copy-start.1 = (bf16[2,1,128,1024]{3,2,1,0:T(8,128)(2,1)S(1)}, bf16[2,1,128,1024]{3,2,1,0:T(8,128)(2,1)}, u32[]{:S(2)}) copy-start(bf16[2,1,128,1024]{3,2,1,0:T(8,128)(2,1)} %param.2) | copy-start | bytes 1572868
  0.0 15.2 %collective-permute-start = (bf16[2,1,128,1024]{3,2,1,0:T(8,128)(2,1)}, bf16[2,1,128,1024]{3,2,1,0:T(8,128)(2,1)S(1)}, u32[]{:S(2)}, u32[]{:S(2)}) collective-permute-start(bf16[2,1,128,1024]{3,2,1,0:T(8,128)(2,1)} %param.2), channel_id=1, source_target_pairs={{1,0},{2,1},{3,2},{4,3},{5,4},{6,5},{7,6},{8,7},{9,8},{10,9},{11,1... | collective-permute-start | bytes 1572872 | tf_op jit(solution)/shard_map/ppermute | solution.py:14
  0.7 17.9 %collective-permute-start.1 = (bf16[2,1,128,1024]{3,2,1,0:T(8,128)(2,1)}, bf16[2,1,128,1024]{3,2,1,0:T(8,128)(2,1)S(1)}, u32[]{:S(2)}, u32[]{:S(2)}) collective-permute-start(bf16[2,1,128,1024]{3,2,1,0:T(8,128)(2,1)} %param.2), channel_id=1, source_target_pairs={{2,0},{3,1},{4,2},{5,3},{6,4},{7,5},{8,6},{9,7},{10,8},{11,9},{12,... | collective-permute-start | bytes 1572872 | tf_op jit(solution)/shard_map/ppermute | solution.py:14
  0.9 38.0 %collective-permute-start.2 = (bf16[2,1,128,1024]{3,2,1,0:T(8,128)(2,1)}, bf16[2,1,128,1024]{3,2,1,0:T(8,128)(2,1)}, u32[]{:S(2)}, u32[]{:S(2)}) collective-permute-start(bf16[2,1,128,1024]{3,2,1,0:T(8,128)(2,1)} %param.2), channel_id=1, source_target_pairs={{5,0},{6,1},{7,2},{8,3},{9,4},{10,5},{11,6},{12,7},{13,8},{14,9},{... | collective-permute-start | bytes 1572872 | tf_op jit(solution)/shard_map/ppermute | solution.py:14
  5.2 48.4 %collective-permute-start.3 = (bf16[2,1,128,1024]{3,2,1,0:T(8,128)(2,1)}, bf16[2,1,128,1024]{3,2,1,0:T(8,128)(2,1)}, u32[]{:S(2)}, u32[]{:S(2)}) collective-permute-start(bf16[2,1,128,1024]{3,2,1,0:T(8,128)(2,1)} %param.2), channel_id=1, source_target_pairs={{8,0},{9,1},{10,2},{11,3},{12,4},{13,5},{14,6},{15,7},{0,8},{1,9},... | collective-permute-start | bytes 1572872 | tf_op jit(solution)/shard_map/ppermute | solution.py:14
  18.6 23.9 %copy-start.3 = (bf16[2,1,128,1024]{3,2,1,0:T(8,128)(2,1)}, bf16[2,1,128,1024]{3,2,1,0:T(8,128)(2,1)S(1)}, u32[]{:S(2)}) copy-start(bf16[2,1,128,1024]{3,2,1,0:T(8,128)(2,1)S(1)} %collective-permute-done.1) | copy-start | bytes 1572868
  53.6 1.4 %copy-start.4 = (bf16[2,1,128,1024]{3,2,1,0:T(8,128)(2,1)S(1)}, bf16[2,1,128,1024]{3,2,1,0:T(8,128)(2,1)}, u32[]{:S(2)}) copy-start(bf16[2,1,128,1024]{3,2,1,0:T(8,128)(2,1)} %copy-done.3) | copy-start | bytes 1572868
  63.6 1.4 %copy-start.2 = (bf16[2,1,128,1024]{3,2,1,0:T(8,128)(2,1)S(1)}, bf16[2,1,128,1024]{3,2,1,0:T(8,128)(2,1)}, u32[]{:S(2)}) copy-start(bf16[2,1,128,1024]{3,2,1,0:T(8,128)(2,1)} %param.2) | copy-start | bytes 1572868
  70.9 23.7 %copy-start = (s32[136]{0:T(256)S(1)}, s32[136]{0:T(256)}, u32[]{:S(2)}) copy-start(s32[136]{0:T(256)} %constant.111) | copy-start | bytes 1636
  70.9 51.4 %all-to-all-start = ((f32[2,1,1,9,128,128]{5,0,3,2,1,4:T(2,128)}), f32[2,1,1,9,128,128]{5,0,3,2,1,4:T(2,128)S(1)}, u32[]{:S(2)}, u32[]{:S(2)}) async-start(f32[2,1,1,9,128,128]{5,0,3,2,1,4:T(2,128)} %copy.171), calls=%async_computation | async-start | bytes 2359296 | tf_op jit(solution)/shard_map/all_to_all | solution.py:111
where the time goes:
time: 125 us; the launch traced here: 124 us
  waiting for transfers between devices  55 us (44%)
  matrix products  34.5 us (28%)
  starting transfers between devices  28.9 us (23%)
  local copies, waits for them, and re-layouts  4.71 us (4%)
    all_to_all x1, waiting for transfers between devices, on_device(): lax.all_to_all(tile_slots[:, None], 'tile', split_axis=4, concat_axis=1,...  27.7 us
    ppermute x4, waiting for transfers between devices, passed_along(): return lax.ppermute(block, axis, route)  27.3 us
    all_to_all x1, starting transfers between devices, on_device(): lax.all_to_all(tile_slots[:, None], 'tile', split_axis=4, concat_axis=1,...  23.7 us
    dot_general x9, matrix products, pair_tile(): jnp.einsum('cit,cjt->cij', rows_side[1], cols_side[1], preferred_element_...  9.05 us
    dot_general x9, matrix products, pair_tile(): jnp.einsum('cit,cjt->cij', rows_side[0], cols_side[0], preferred_element_...  8.85 us
    dot_general x9, matrix products, pair_tile(): jnp.einsum('cit,cjt->cij', rows_side[1], cols_side[0], preferred_element_...  8.8 us
    dot_general x9, matrix products, pair_tile(): jnp.einsum('cit,cjt->cij', rows_side[0], cols_side[1], preferred_element_...  7.76 us
    ppermute x4, starting transfers between devices, passed_along(): return lax.ppermute(block, axis, route)  5.24 us
  transfers between devices with their start and end apart: 5, of which 4 were waited for; matrix products, arithmetic and copies ran while one was open for 17% of the time, Pallas kernels for 0%

commit v1 on v0

--- a/solution.py
+++ b/solution.py
@@ -108,7 +108,16 @@
         second_block = (own_block + second_member) % NBLK
         tiles_list.append(jnp.where(first_block < second_block, product, flipped))
     tile_slots = jnp.stack(tiles_list, axis=2)
-    received = lax.all_to_all(tile_slots[:, None], "tile", split_axis=4, concat_axis=1, tiled=True)
+    inp = tile_slots[:, None]
+    received = jnp.concatenate(
+        lax.all_to_all(
+            jnp.stack(jnp.split(inp, lax.axis_size("tile"), axis=4)),
+            axis_name="tile",
+            split_axis=0,
+            concat_axis=0,
+        ),
+        axis=1,
+    )
     return channel_order(received, NBLK // 2 + 1, cover_sources(NBLK // 2 + 1, members))
 
 

time: 125 us -> 133 us (1.064)
  local copies, waits for them, and re-layouts: 4.71 us -> 12.9 us
    unnamed x10 -> x25, local copies, waits for them, and re-layouts: 0.02 us -> 9.63 us
    broadcast_in_dim x1 -> x0, local copies, waits for them, and re-layouts: 1.97 us -> none  [on_device(): tile_slots[:, None]]
  transfers between devices with their start and end apart: 5 -> 5, of which waited for: 4 -> 4; matrix products, arithmetic and copies ran while one was open for 17% -> 16% of each run, Pallas kernels for 0% -> 0%
where the time goes in v1:
time: 133 us; the launch traced here: 132 us
  waiting for transfers between devices  55 us (41%)
  matrix products  34.5 us (26%)
  starting transfers between devices  28.9 us (22%)
  local copies, waits for them, and re-layouts  12.9 us (10%)
    all_to_all x1, waiting for transfers between devices, on_device(): lax.all_to_all(jnp.stack(jnp.split(inp, lax.axis_size('tile'), axis=4)),...  27.7 us
    ppermute x4, waiting for transfers between devices, passed_along(): return lax.ppermute(block, axis, route)  27.3 us
    all_to_all x1, starting transfers between devices, on_device(): lax.all_to_all(jnp.stack(jnp.split(inp, lax.axis_size('tile'), axis=4)),...  23.7 us
    unnamed x25, local copies, waits for them, and re-layouts  9.63 us
    dot_general x9, matrix products, pair_tile(): jnp.einsum('cit,cjt->cij', rows_side[1], cols_side[1], preferred_element_...  9.05 us
    dot_general x9, matrix products, pair_tile(): jnp.einsum('cit,cjt->cij', rows_side[0], cols_side[0], preferred_element_...  8.85 us
    dot_general x9, matrix products, pair_tile(): jnp.einsum('cit,cjt->cij', rows_side[1], cols_side[0], preferred_element_...  8.8 us
    dot_general x9, matrix products, pair_tile(): jnp.einsum('cit,cjt->cij', rows_side[0], cols_side[1], preferred_element_...  7.76 us
  transfers between devices with their start and end apart: 5, of which 4 were waited for; matrix products, arithmetic and copies ran while one was open for 16% of the time, Pallas kernels for 0%

profile of v1, /device:TPU:15, one launch (start us, length us, event | category | flops | bytes accessed | tf_op | source)
XLA Modules:
  0.0 132.5 jit_solution(4183949672873392497)
XLA Ops:
  0.0 0.7 collective-permute-start
  0.7 0.2 collective-permute-start.1
  0.9 4.3 %collective-permute-start.2 = (bf16[2,1,128,1024]{3,2,1,0:T(8,128)(2,1)}, bf16[2,1,128,1024]{3,2,1,0:T(8,128)(2,1)}, u32[]{:S(2)}, u32[]{:S(2)}) collective-permute-start(bf16[2,1,128,1024]{3,2,1,0:T(8,128)(2,1)} %param.2), channel_id=1, source_target_pairs={{5,0},{6,1},{7,2},{8,3},{9,4},{10,5},{11,6},{12,7},{13,8},{14,9},{... | collective-permute-start | bytes 1572872 | tf_op jit(solution)/shard_map/ppermute | solution.py:14
  5.2 1.3 fusion.32
  6.5 1.3 fusion.1
  7.9 1.3 fusion.15
  9.1 0.2 fusion
  9.4 5.8 %collective-permute-done = bf16[2,1,128,1024]{3,2,1,0:T(8,128)(2,1)S(1)} collective-permute-done((bf16[2,1,128,1024]{3,2,1,0:T(8,128)(2,1)}, bf16[2,1,128,1024]{3,2,1,0:T(8,128)(2,1)S(1)}, u32[]{:S(2)}, u32[]{:S(2)}) %collective-permute-start) | collective-permute-done | bytes 524320 | tf_op jit(solution)/shard_map/ppermute | solution.py:14
  15.2 0.2 fusion.12
  15.5 0.2 convolution_add_fusion.7
  15.7 0.2 fusion.27
  15.9 0.2 convolution_subtract_fusion.7
  16.2 0.1 copy.39
  16.3 2.3 %collective-permute-done.1 = bf16[2,1,128,1024]{3,2,1,0:T(8,128)(2,1)S(1)} collective-permute-done((bf16[2,1,128,1024]{3,2,1,0:T(8,128)(2,1)}, bf16[2,1,128,1024]{3,2,1,0:T(8,128)(2,1)S(1)}, u32[]{:S(2)}, u32[]{:S(2)}) %collective-permute-start.1) | collective-permute-done | bytes 524320 | tf_op jit(solution)/shard_map/ppermute | solution.py:14
  18.6 0.2 fusion.9
  18.8 0.2 fusion.24
  19.0 0.2 convolution_add_fusion.6
  19.3 0.2 convolution_subtract_fusion.6
  19.5 0.1 copy.44
  19.7 19.2 %collective-permute-done.2 = bf16[2,1,128,1024]{3,2,1,0:T(8,128)(2,1)} collective-permute-done((bf16[2,1,128,1024]{3,2,1,0:T(8,128)(2,1)}, bf16[2,1,128,1024]{3,2,1,0:T(8,128)(2,1)}, u32[]{:S(2)}, u32[]{:S(2)}) %collective-permute-start.2) | collective-permute-done | bytes 524320 | tf_op jit(solution)/shard_map/ppermute | solution.py:14
  38.9 1.2 fusion.52
  40.1 1.2 fusion.50
  41.3 1.2 convolution_add_fusion.5
  42.5 1.2 convolution_subtract_fusion.5
  43.8 1.2 fusion.48
  45.0 1.2 fusion.46
  46.2 1.2 convolution_add_fusion.4
  47.4 1.2 convolution_subtract_fusion.4
  48.7 1.2 fusion.6
  49.9 1.2 fusion.21
  51.1 1.2 convolution_add_fusion.3
  52.3 1.2 convolution_subtract_fusion.3
  53.7 1.3 fusion.51
  55.0 1.2 fusion.49
  56.2 1.2 convolution_add_fusion.2
  57.4 1.2 convolution_subtract_fusion.2
  58.7 1.2 fusion.47
  59.9 1.2 fusion.45
  61.1 1.2 convolution_add_fusion.1
  62.3 1.2 convolution_subtract_fusion.1
  63.7 1.3 fusion.3
  65.0 1.2 fusion.18
  66.2 1.2 convolution_add_fusion
  67.4 1.2 convolution_subtract_fusion
  68.9 0.7 fusion.68
  69.6 0.6 fusion.67
  70.2 0.6 fusion.66
  70.9 0.6 fusion.65
  71.5 0.6 fusion.64
  72.1 0.6 fusion.63
  72.8 0.6 fusion.62
  73.4 0.6 fusion.61
  74.1 0.6 fusion.60
  74.7 0.7 fusion.59
  75.3 0.7 fusion.58
  76.0 0.6 fusion.57
  76.6 0.6 fusion.56
  77.3 0.6 fusion.55
  77.9 0.6 fusion.54
  78.6 0.6 fusion.53
  79.2 23.7 %all-to-all-start = ((f32[16,2,1,1,9,8,128]{6,5,4,1,3,2,0:T(8,128)}), f32[16,2,1,1,9,8,128]{6,5,4,1,3,2,0:T(8,128)S(1)}, u32[]{:S(2)}, u32[]{:S(2)}) async-start(f32[16,2,1,1,9,8,128]{6,5,4,1,3,2,0:T(8,128)} %fusion.53), calls=%async_computation | async-start | bytes 2359296 | tf_op jit(solution)/shard_map/all_to_all | solution.py:113
  102.9 27.7 %all-to-all-done = f32[16,2,1,1,9,8,128]{6,5,4,1,3,2,0:T(8,128)S(1)} async-done(((f32[16,2,1,1,9,8,128]{6,5,4,1,3,2,0:T(8,128)}), f32[16,2,1,1,9,8,128]{6,5,4,1,3,2,0:T(8,128)S(1)}, u32[]{:S(2)}, u32[]{:S(2)}) %all-to-all-start) | async-done | bytes 1179680 | tf_op jit(solution)/shard_map/all_to_all | solution.py:113
  130.7 0.7 gather_fusion
  131.4 1.1 copy.68
  (53 shorter events, 1.1 us)
Async XLA Ops:
  0.0 9.1 %copy-start.1 = (bf16[2,1,128,1024]{3,2,1,0:T(8,128)(2,1)S(1)}, bf16[2,1,128,1024]{3,2,1,0:T(8,128)(2,1)}, u32[]{:S(2)}) copy-start(bf16[2,1,128,1024]{3,2,1,0:T(8,128)(2,1)} %param.2) | copy-start | bytes 1572868
  0.0 15.2 %collective-permute-start = (bf16[2,1,128,1024]{3,2,1,0:T(8,128)(2,1)}, bf16[2,1,128,1024]{3,2,1,0:T(8,128)(2,1)S(1)}, u32[]{:S(2)}, u32[]{:S(2)}) collective-permute-start(bf16[2,1,128,1024]{3,2,1,0:T(8,128)(2,1)} %param.2), channel_id=1, source_target_pairs={{1,0},{2,1},{3,2},{4,3},{5,4},{6,5},{7,6},{8,7},{9,8},{10,9},{11,1... | collective-permute-start | bytes 1572872 | tf_op jit(solution)/shard_map/ppermute | solution.py:14
  0.7 17.9 %collective-permute-start.1 = (bf16[2,1,128,1024]{3,2,1,0:T(8,128)(2,1)}, bf16[2,1,128,1024]{3,2,1,0:T(8,128)(2,1)S(1)}, u32[]{:S(2)}, u32[]{:S(2)}) collective-permute-start(bf16[2,1,128,1024]{3,2,1,0:T(8,128)(2,1)} %param.2), channel_id=1, source_target_pairs={{2,0},{3,1},{4,2},{5,3},{6,4},{7,5},{8,6},{9,7},{10,8},{11,9},{12,... | collective-permute-start | bytes 1572872 | tf_op jit(solution)/shard_map/ppermute | solution.py:14
  0.9 38.0 %collective-permute-start.2 = (bf16[2,1,128,1024]{3,2,1,0:T(8,128)(2,1)}, bf16[2,1,128,1024]{3,2,1,0:T(8,128)(2,1)}, u32[]{:S(2)}, u32[]{:S(2)}) collective-permute-start(bf16[2,1,128,1024]{3,2,1,0:T(8,128)(2,1)} %param.2), channel_id=1, source_target_pairs={{5,0},{6,1},{7,2},{8,3},{9,4},{10,5},{11,6},{12,7},{13,8},{14,9},{... | collective-permute-start | bytes 1572872 | tf_op jit(solution)/shard_map/ppermute | solution.py:14
  5.2 48.4 %collective-permute-start.3 = (bf16[2,1,128,1024]{3,2,1,0:T(8,128)(2,1)}, bf16[2,1,128,1024]{3,2,1,0:T(8,128)(2,1)}, u32[]{:S(2)}, u32[]{:S(2)}) collective-permute-start(bf16[2,1,128,1024]{3,2,1,0:T(8,128)(2,1)} %param.2), channel_id=1, source_target_pairs={{8,0},{9,1},{10,2},{11,3},{12,4},{13,5},{14,6},{15,7},{0,8},{1,9},... | collective-permute-start | bytes 1572872 | tf_op jit(solution)/shard_map/ppermute | solution.py:14
  18.6 23.9 %copy-start.3 = (bf16[2,1,128,1024]{3,2,1,0:T(8,128)(2,1)}, bf16[2,1,128,1024]{3,2,1,0:T(8,128)(2,1)S(1)}, u32[]{:S(2)}) copy-start(bf16[2,1,128,1024]{3,2,1,0:T(8,128)(2,1)S(1)} %collective-permute-done.1) | copy-start | bytes 1572868
  53.6 1.4 %copy-start.4 = (bf16[2,1,128,1024]{3,2,1,0:T(8,128)(2,1)S(1)}, bf16[2,1,128,1024]{3,2,1,0:T(8,128)(2,1)}, u32[]{:S(2)}) copy-start(bf16[2,1,128,1024]{3,2,1,0:T(8,128)(2,1)} %copy-done.3) | copy-start | bytes 1572868
  63.6 1.4 %copy-start.2 = (bf16[2,1,128,1024]{3,2,1,0:T(8,128)(2,1)S(1)}, bf16[2,1,128,1024]{3,2,1,0:T(8,128)(2,1)}, u32[]{:S(2)}) copy-start(bf16[2,1,128,1024]{3,2,1,0:T(8,128)(2,1)} %param.2) | copy-start | bytes 1572868
  79.2 23.7 %copy-start = (s32[136]{0:T(256)S(1)}, s32[136]{0:T(256)}, u32[]{:S(2)}) copy-start(s32[136]{0:T(256)} %constant.111) | copy-start | bytes 1636
  79.2 51.4 %all-to-all-start = ((f32[16,2,1,1,9,8,128]{6,5,4,1,3,2,0:T(8,128)}), f32[16,2,1,1,9,8,128]{6,5,4,1,3,2,0:T(8,128)S(1)}, u32[]{:S(2)}, u32[]{:S(2)}) async-start(f32[16,2,1,1,9,8,128]{6,5,4,1,3,2,0:T(8,128)} %fusion.53), calls=%async_computation | async-start | bytes 2359296 | tf_op jit(solution)/shard_map/all_to_all | solution.py:113
